TPU v7x, 128 devices: a whole 4x4x4 slice. The times are simulated.
128 devices in a mesh: rows: 16 (over z_hi, x, core), cols: 8 (over y, z_lo).
Axes of the slice: x: 4, y: 4, z: 4 (z_hi: 2, z_lo: 2; z = z_hi * 2 + z_lo), core: 2. Of those that a mesh axis runs over, the one named last changes fastest.
Arguments:
- block_values: bfloat16 [65536, 128], P(('rows', 'cols')), may hold values from -6 to 6
- block_length: int32 [65536], P(('rows', 'cols')), may hold values from 1 to 128
- block_owner: int32 [65536], P(('rows', 'cols')), may hold values from 0 to 16383, as said below
- block_second: int32 [65536], P(('rows', 'cols')), may hold values from 0 to 16383, as said below
- block_third: int32 [65536, 128], P(('rows', 'cols')), may hold values from 0 to 32767
- live_blocks: int32 [128], P(('rows', 'cols')), may hold values from 1 to 512, as said below
- second_factor: bfloat16 [16384, 256], P('cols', 'rows')
- third_factor: bfloat16 [32768, 256], P('cols', 'rows'), may hold values from -6 to 6
Outputs:
- first_factor: float32 [16384, 256], P('cols', 'rows')
Inputs may be any that keep to these rules, and one draw needn't show every extreme that they name: `block_owner`: slot b lies on device d = b // 512 with index r along rows; its row lies in r * 16384 // 16 up to (r + 1) * 16384 // 16 - 1, the device's mode-1 slab. `block_second`: slot b lies on device d = b // 512 with index c along cols; its row lies in c * 16384 // 8 up to (c + 1) * 16384 // 8 - 1. `live_blocks`: some device uses all 512 slots in every draw.
All inputs are finite; a program needn't handle non-finite values.
Results may differ from a plain program's by a relative error of at most 0.0003.
Values may be sent and summed in bfloat16 or wider, within the bound.
No kernel may reach another device: no remote copies, remote signals or barrier semaphores. Data moves between devices by JAX's collectives and lax.ppermute only.
A program may use at most 128 MiB of HBM per device.

v0:
```python
import jax
import jax.numpy as jnp
from jax import lax
from jax.sharding import PartitionSpec as P

I_DEV = 128


def joined_along(blocks, dim):
    shape = list(blocks.shape[1:])
    shape[dim] *= blocks.shape[0]
    return jnp.moveaxis(blocks, 0, dim).reshape(shape)


def from_everyone(value, axis):
    size = lax.axis_size(axis)
    return lax.all_to_all(
        jnp.broadcast_to(value[None], (size, *value.shape)), axis, 0, 0, tiled=True
    )


def collect(value, axis, dim):
    return joined_along(from_everyone(value, axis), dim)


def gram_product(left, right):
    contract = (((0,), (0,)), ((), ()))
    return lax.dot_general(left, right, contract, preferred_element_type=jnp.float32)


def block_fold(values, third, table):
    group = values.shape[0]
    width = values.shape[1]
    picked = table[third.reshape(group * width)]
    scaled = values.reshape(group * width, 1).astype(jnp.float32) * picked.astype(jnp.float32)
    return jnp.sum(scaled.reshape(group, width, picked.shape[1]), axis=1)


def per_device(
    block_values,
    block_length,
    block_owner,
    block_second,
    block_third,
    live_blocks,
    second_factor,
    third_factor,
):
    n_rows = lax.axis_size("rows")
    n_cols = lax.axis_size("cols")
    row_at = lax.axis_index("rows")
    col_at = lax.axis_index("cols")
    contract = (((0,), (0,)), ((), ()))
    width = block_values.shape[1]
    lane = jnp.arange(width, dtype=jnp.int32)
    slab = I_DEV * n_cols
    owned = jnp.arange(slab, dtype=jnp.int32)
    second_range = lax.all_gather(second_factor, "rows", axis=1, tiled=True)
    third_part = collect(third_factor, "cols", 0)
    third_whole = lax.all_gather(third_part, "rows", axis=1, tiled=True)
    range_rows = second_range.shape[0]
    local_gram = gram_product(second_range, second_range)
    gram_second = lax.psum(local_gram, "cols") / (range_rows * n_cols)
    gram_third = gram_product(third_whole, third_whole) / third_whole.shape[0]
    gram = gram_second * gram_third
    nblk = block_values.shape[0]
    group = min(nblk, 128)
    count = live_blocks[0]

    def accumulate(step, total):
        start = step * group
        values = lax.dynamic_slice_in_dim(block_values, start, group, 0)
        lengths = lax.dynamic_slice_in_dim(block_length, start, group, 0)
        third = lax.dynamic_slice_in_dim(block_third, start, group, 0)
        second = lax.dynamic_slice_in_dim(block_second, start, group, 0)
        owner = lax.dynamic_slice_in_dim(block_owner, start, group, 0)
        slot = start + jnp.arange(group, dtype=jnp.int32)
        live = (lane[None, :] < lengths[:, None]) & (slot < count)[:, None]
        values = jnp.where(live, values, jnp.zeros((), jnp.bfloat16))
        fold = block_fold(values, third, third_whole)
        contrib = second_range[second - col_at * range_rows].astype(jnp.float32) * fold
        onehot = ((owner - row_at * slab)[:, None] == owned[None, :]).astype(jnp.float32)
        return total + lax.dot_general(
            onehot,
            contrib,
            contract,
            precision=lax.Precision.HIGHEST,
            preferred_element_type=jnp.float32,
        )

    start_total = jnp.zeros((slab, gram.shape[0]), jnp.float32)
    partial_rows = lax.fori_loop(0, nblk // group, accumulate, start_total)
    mine = lax.psum_scatter(partial_rows, "cols", scatter_dimension=0, tiled=True)
    factor = jnp.linalg.cholesky(gram)
    solved = jax.scipy.linalg.cho_solve((factor, True), mine.T).T
    moved = lax.all_to_all(
        lax.all_to_all(solved, "rows", split_axis=1, concat_axis=0, tiled=True),
        "cols",
        split_axis=0,
        concat_axis=0,
        tiled=True,
    )
    share = n_rows // n_cols
    owned_rows = mine.shape[0]
    reordered = moved.reshape(n_cols, share, owned_rows, moved.shape[1]).transpose(1, 0, 2, 3)
    return reordered.reshape(n_rows * owned_rows, moved.shape[1])


def solution(mesh):
    return jax.shard_map(
        per_device,
        mesh=mesh,
        in_specs=(
            P(("rows", "cols"), None),
            P(("rows", "cols")),
            P(("rows", "cols")),
            P(("rows", "cols")),
            P(("rows", "cols"), None),
            P(("rows", "cols")),
            P("cols", "rows"),
            P("cols", "rows"),
        ),
        out_specs=P("cols", "rows"),
        check_vma=False,
    )
```

profile of v0, /device:TPU:0, one launch (start us, length us, event | category | flops | bytes accessed | tf_op | source)
XLA Modules:
  0.0 622.8 jit_solution(15795296984549790997)
XLA Ops:
  7.3 1.0 broadcast_in_dim.48
  8.3 21.1 %all_to_all.30 = bf16[8,4096,16]{1,2,0:T(8,128)(2,1)S(1)} all-to-all(bf16[8,4096,16]{1,2,0:T(8,128)(2,1)S(1)} %broadcast_in_dim.48), channel_id=1, replica_groups=mesh['rows'=16,'cols'=8] {'cols'}, dimensions={0} | all-to-all | bytes 2097152 | tf_op jit(solution)/shard_map/all_to_all | solution.py:17
  29.4 1.1 copy.51
  30.6 28.7 %all-gather.3.cloned.1.call-done = bf16[2048,256]{0,1:T(8,128)(2,1)} async-done(((bf16[2048,16]{0,1:T(8,128)(2,1)}), bf16[2048,256]{0,1:T(8,128)(2,1)}) %all-gather.3.cloned.1.call-update) | async-done | bytes 1048592 | tf_op jit(solution)/shard_map/all_gather | solution.py:58
  59.3 2.8 fusion.24
  62.1 1.5 copy.43
  63.6 106.5 %all-gather.5.cloned.1.call-done = bf16[32768,256]{0,1:T(8,128)(2,1)} async-done(((bf16[32768,16]{0,1:T(8,128)(2,1)}), bf16[32768,256]{0,1:T(8,128)(2,1)}) %all-gather.5.cloned.1.call-update) | async-done | bytes 16777232 | tf_op jit(solution)/shard_map/all_gather | solution.py:60
  170.2 22.4 %copy.44 = bf16[32768,256]{1,0:T(8,128)(2,1)} copy(bf16[32768,256]{0,1:T(8,128)(2,1)} %all-gather.5.cloned.1.call-done) | data formatting | bytes 33554432
  192.6 321.0 %while.18 = (s32[]{:T(128)}, f32[1024,256]{1,0:T(8,128)S(1)}, s32[512]{0:T(512)}, s32[]{:T(128)}, s32[512]{0:T(512)}, /*index=5*/s32[]{:T(128)}, bf16[2048,256]{...) while((s32[]{:T(128)}, f32[1024,256]{1,0:T(8,128)S(1)}, ...), condition=%wide.region_7.8_spmd.clone, body=%wide.region_5.7_spmd.clone.sunk | while | flops 416057216 | bytes 28354028 | solution.py:92
  194.0 0.9 fusion.42
  194.8 0.9 constant_dynamic-slice_fusion.5
  195.8 68.7 %gather_fusion = bf16[16384,256]{1,0:T(8,128)(2,1)} fusion(bf16[32768,256]{1,0:T(8,128)(2,1)} %get-tuple-element.593, s32[16384]{0:T(1024)S(1)} %broadcast_clamp_fusion.2), kind=kCustom, calls=%fused_computation.1.clone.clone.1 | custom fusion | bytes 16842752 | tf_op jit(solution)/shard_map/while/body/eval_jaxpr/gather | solution.py:34
  264.5 5.5 fusion.43
  269.9 0.8 compare_select_fusion.4
  270.7 0.8 gather_fusion.1
  271.6 1.2 convolution_add_fusion.2
  274.2 0.9 fusion.42
  275.1 0.9 constant_dynamic-slice_fusion.5
  276.0 68.7 %gather_fusion = bf16[16384,256]{1,0:T(8,128)(2,1)} fusion(bf16[32768,256]{1,0:T(8,128)(2,1)} %get-tuple-element.593, s32[16384]{0:T(1024)S(1)} %broadcast_clamp_fusion.2), kind=kCustom, calls=%fused_computation.1.clone.clone.1 | custom fusion | bytes 16842752 | tf_op jit(solution)/shard_map/while/body/eval_jaxpr/gather | solution.py:34
  344.7 5.5 fusion.43
  350.1 0.8 compare_select_fusion.4
  350.9 0.8 gather_fusion.1
  351.8 1.2 convolution_add_fusion.2
  354.4 0.9 fusion.42
  355.3 0.9 constant_dynamic-slice_fusion.5
  356.2 68.7 %gather_fusion = bf16[16384,256]{1,0:T(8,128)(2,1)} fusion(bf16[32768,256]{1,0:T(8,128)(2,1)} %get-tuple-element.593, s32[16384]{0:T(1024)S(1)} %broadcast_clamp_fusion.2), kind=kCustom, calls=%fused_computation.1.clone.clone.1 | custom fusion | bytes 16842752 | tf_op jit(solution)/shard_map/while/body/eval_jaxpr/gather | solution.py:34
  424.9 5.5 fusion.43
  431.1 0.8 gather_fusion.1
  432.0 1.2 convolution_add_fusion.2
  434.6 0.9 fusion.42
  435.5 0.9 constant_dynamic-slice_fusion.5
  436.4 68.7 %gather_fusion = bf16[16384,256]{1,0:T(8,128)(2,1)} fusion(bf16[32768,256]{1,0:T(8,128)(2,1)} %get-tuple-element.593, s32[16384]{0:T(1024)S(1)} %broadcast_clamp_fusion.2), kind=kCustom, calls=%fused_computation.1.clone.clone.1 | custom fusion | bytes 16842752 | tf_op jit(solution)/shard_map/while/body/eval_jaxpr/gather | solution.py:34
  505.1 5.5 fusion.43
  511.4 0.8 gather_fusion.1
  512.2 1.2 convolution_add_fusion.2
  513.6 1.3 copy.45
  515.0 15.2 %fusion.11 = f32[256,256]{0,1:T(8,128)S(1)} fusion(bf16[32768,256]{0,1:T(8,128)(2,1)} %all-gather.5.cloned.1.call-done, f32[256,256]{0,1:T(8,128)} %all-reduce.3.cloned.1.call-done), kind=kOutput, calls=%fused_computation.25 | convolution fusion | flops 4295163904 | bytes 17301504 | tf_op jit(solution)/shard_map/dot_general | solution.py:28
  530.3 11.7 %cholesky.50 = f32[128,128]{1,0:T(8,128)S(1)} custom-call(f32[128,128]{1,0:T(8,128)S(1)} %cholesky.118), custom_call_target="Cholesky" | custom-call | tf_op jit(solution)/shard_map/jit(cholesky)/cholesky | solution.py:94
  542.1 9.8 %custom-call.18 = f32[1,128,128]{1,2,0:T(8,128)S(1)} custom-call(f32[1,128,128]{2,1,0:T(8,128)S(1)} %get-tuple-element.439), custom_call_target="InvertDiagBlocksLowerTriangular" | custom-call | tf_op jit(solution)/shard_map/jit(cholesky)/cholesky | solution.py:94
  552.4 11.9 %cholesky.105 = f32[128,128]{1,0:T(8,128)S(1)} custom-call(f32[128,128]{1,0:T(8,128)S(1)} %convolution_subtract_fusion.2), custom_call_target="Cholesky" | custom-call | tf_op jit(solution)/shard_map/jit(cholesky)/cholesky | solution.py:94
  566.5 4.1 while.17
  567.1 1.3 bitcast_dynamic-update-slice_fusion.2
  569.2 1.3 bitcast_dynamic-update-slice_fusion.2
  570.5 19.7 %custom-call.19 = f32[2,128,128]{1,2,0:T(8,128)S(1)} custom-call(f32[2,128,128]{2,1,0:T(8,128)S(1)} %get-tuple-element.332), custom_call_target="InvertDiagBlocksLowerTriangular" | custom-call | tf_op jit(solution)/shard_map/jit(_cho_solve)/triangular_solve | solution.py:95
  590.2 1.1 fusion.13
  591.4 1.0 convolution_subtract_fusion.1
  593.5 10.6 %all_to_all.31 = f32[128,16,16]{0,2,1:T(8,128)S(1)} all-to-all(f32[128,16,16]{0,2,1:T(8,128)S(1)} %bitcast.75), channel_id=1, replica_groups=mesh['rows'=16,'cols'=8] {'rows'}, dimensions={1} | all-to-all | bytes 262144 | tf_op jit(solution)/shard_map/all_to_all | solution.py:97
  604.2 11.2 %all_to_all.32 = f32[8,256,16]{1,2,0:T(8,128)S(1)} all-to-all(f32[8,256,16]{1,2,0:T(8,128)S(1)} %copy.47), channel_id=1, replica_groups=mesh['rows'=16,'cols'=8] {'cols'}, dimensions={0} | all-to-all | bytes 262144 | tf_op jit(solution)/shard_map/all_to_all | solution.py:96
  (61 shorter events, 13.3 us)
Async XLA Ops:
  6.5 52.8 %all-gather.3.cloned.1.call-start = ((), (), s32[]{:S(2)}) async-start(), calls=%async_computation.4 | async-start | bytes 1114112 | tf_op jit(solution)/shard_map/all_gather | solution.py:58
  7.3 162.9 %all-gather.5.cloned.1.call-start = ((), (), s32[]{:S(2)}) async-start(), calls=%async_computation.6 | async-start | bytes 17825792 | tf_op jit(solution)/shard_map/all_gather | solution.py:60
  30.5 484.4 %all-reduce.3.cloned.1.call-start = ((), (), s32[]{:S(2)}) async-start(), calls=%async_computation.5 | async-start | bytes 524288 | tf_op jit(solution)/shard_map/psum | solution.py:63
  62.1 528.1 %reduce-scatter.2.cloned.1.call-start = ((), (), s32[]{:S(2)}) async-start(), calls=%async_computation.7 | async-start | bytes 1179648 | tf_op jit(solution)/shard_map/reduce_scatter | solution.py:93
Sparse Core Ops, SparseCore 0:
  9.8 49.4 all-gather.2
  61.7 108.3 all-gather.4
  172.6 71.8 all-reduce.2
  515.1 37.6 reduce-scatter.1
where the time goes:
time: 625 us; the launch traced here: 623 us
  local copies, waits for them, and re-layouts  317 us (51%)
  waiting for transfers between devices  136 us (22%)
  other arithmetic  85.4 us (14%)
  blocking collectives  42.9 us (7%)
  matrix products  26.3 us (4%)
  between operations  14.6 us (2%)
    gather x4, local copies, waits for them, and re-layouts, block_fold(): picked = table[third.reshape(group * width)]  275 us
    all_gather x1, waiting for transfers between devices, per_device(): third_whole = lax.all_gather(third_part, 'rows', axis=1, tiled=True)  107 us
    another operation x6, other arithmetic, per_device(): factor = jnp.linalg.cholesky(gram)  34.2 us
    all_gather x1, waiting for transfers between devices, per_device(): second_range = lax.all_gather(second_factor, 'rows', axis=1, tiled=True)  28.7 us
    unnamed x3, local copies, waits for them, and re-layouts  24.6 us
    reduce_sum x4, other arithmetic, block_fold(): return jnp.sum(scaled.reshape(group, width, picked.shape[1]), axis=1)  21.8 us
    all_to_all x1, blocking collectives, from_everyone(): lax.all_to_all(jnp.broadcast_to(value[None], (size, *value.shape)), axis,...  21.1 us
    another operation x4, other arithmetic, per_device(): solved = jax.scipy.linalg.cho_solve((factor, True), mine.T).T  19.7 us
  transfers between devices with their start and end apart: 4, of which 2 were waited for; matrix products, arithmetic and copies ran while one was open for 68% of the time, Pallas kernels for 0%

commit v1 on v0

--- a/solution.py
+++ b/solution.py
@@ -57,7 +57,9 @@
     owned = jnp.arange(slab, dtype=jnp.int32)
     second_range = lax.all_gather(second_factor, "rows", axis=1, tiled=True)
     third_part = collect(third_factor, "cols", 0)
-    third_whole = lax.all_gather(third_part, "rows", axis=1, tiled=True)
+    third_whole = jnp.concatenate(
+        lax.all_to_all(jnp.stack([third_part] * lax.axis_size("rows")), "rows", 0, 0), axis=1
+    )
     range_rows = second_range.shape[0]
     local_gram = gram_product(second_range, second_range)
     gram_second = lax.psum(local_gram, "cols") / (range_rows * n_cols)

time: 625 us -> 725 us (1.16)
  waiting for transfers between devices: 136 us -> 223 us
  starting transfers between devices: 0.12 us -> 7.59 us
    all_gather x1, waiting for transfers between devices: 28.7 us -> 171 us  [per_device(): second_range = lax.all_gather(second_factor, 'rows', axis=1, tiled=True)]
    all_gather x1 -> x0, waiting for transfers between devices: 107 us -> none  [per_device(): third_whole = lax.all_gather(third_part, 'rows', axis=1, tiled=True)]
    all_to_all x0 -> x1, waiting for transfers between devices: none -> 50.5 us  [per_device(): lax.all_to_all(jnp.stack([third_part] * lax.axis_size('rows')), 'rows', 0...]
    all_to_all x0 -> x1, starting transfers between devices: none -> 7.47 us  [per_device(): lax.all_to_all(jnp.stack([third_part] * lax.axis_size('rows')), 'rows', 0...]
  transfers between devices with their start and end apart: 4 -> 4, of which waited for: 2 -> 2; matrix products, arithmetic and copies ran while one was open for 68% -> 58% of each run, Pallas kernels for 0% -> 0%
where the time goes in v1:
time: 725 us; the launch traced here: 723 us
  local copies, waits for them, and re-layouts  322 us (44%)
  waiting for transfers between devices  223 us (31%)
  other arithmetic  85.4 us (12%)
  blocking collectives  44.3 us (6%)
  matrix products  26.2 us (4%)
  between operations  14.6 us (2%)
  starting transfers between devices  7.59 us (1%)
    gather x4, local copies, waits for them, and re-layouts, block_fold(): picked = table[third.reshape(group * width)]  275 us
    all_gather x1, waiting for transfers between devices, per_device(): second_range = lax.all_gather(second_factor, 'rows', axis=1, tiled=True)  171 us
    all_to_all x1, waiting for transfers between devices, per_device(): lax.all_to_all(jnp.stack([third_part] * lax.axis_size('rows')), 'rows', 0...  50.5 us
    another operation x6, other arithmetic, per_device(): factor = jnp.linalg.cholesky(gram)  34.2 us
    unnamed x3, local copies, waits for them, and re-layouts  24.6 us
    reduce_sum x4, other arithmetic, block_fold(): return jnp.sum(scaled.reshape(group, width, picked.shape[1]), axis=1)  21.8 us
    all_to_all x1, blocking collectives, from_everyone(): lax.all_to_all(jnp.broadcast_to(value[None], (size, *value.shape)), axis,...  21.1 us
    another operation x4, other arithmetic, per_device(): solved = jax.scipy.linalg.cho_solve((factor, True), mine.T).T  19.7 us
  transfers between devices with their start and end apart: 4, of which 2 were waited for; matrix products, arithmetic and copies ran while one was open for 58% of the time, Pallas kernels for 0%

profile of v1, /device:TPU:0, one launch (start us, length us, event | category | flops | bytes accessed | tf_op | source)
XLA Modules:
  0.0 723.1 jit_solution(1200105981704761342)
XLA Ops:
  6.5 1.0 broadcast_in_dim.48
  7.5 21.1 %all_to_all.35 = bf16[8,4096,16]{1,2,0:T(8,128)(2,1)S(1)} all-to-all(bf16[8,4096,16]{1,2,0:T(8,128)(2,1)S(1)} %broadcast_in_dim.48), channel_id=1, replica_groups=mesh['rows'=16,'cols'=8] {'cols'}, dimensions={0} | all-to-all | bytes 2097152 | tf_op jit(solution)/shard_map/all_to_all | solution.py:17
  28.7 5.9 stack.3
  34.6 7.5 %all-to-all-start.1 = ((bf16[16,32768,16]{1,2,0:T(8,128)(2,1)}), bf16[16,32768,16]{1,2,0:T(8,128)(2,1)}, u32[]{:S(2)}, u32[]{:S(2)}) async-start(bf16[16,32768,16]{1,2,0:T(8,128)(2,1)} %stack.3), calls=%async_computation.1 | async-start | bytes 33554432 | tf_op jit(solution)/shard_map/all_to_all | solution.py:61
  42.9 171.3 %all-gather.2.cloned.1.call-done = bf16[2048,256]{0,1:T(8,128)(2,1)} async-done(((bf16[2048,16]{0,1:T(8,128)(2,1)}), bf16[2048,256]{0,1:T(8,128)(2,1)}) %all-gather.2.cloned.1.call-update) | async-done | bytes 1048592 | tf_op jit(solution)/shard_map/all_gather | solution.py:58
  214.2 2.7 fusion.24
  217.0 1.5 copy.43
  218.5 50.5 %all-to-all-done.1 = bf16[16,32768,16]{1,2,0:T(8,128)(2,1)} async-done(((bf16[16,32768,16]{1,2,0:T(8,128)(2,1)}), bf16[16,32768,16]{1,2,0:T(8,128)(2,1)}, u32[]{:S(2)}, u32[]{:S(2)}) %all-to-all-start.1) | async-done | bytes 16777248 | tf_op jit(solution)/shard_map/all_to_all | solution.py:61
  269.0 22.4 %copy.44 = bf16[32768,256]{1,0:T(8,128)(2,1)} copy(bf16[32768,256]{0,1:T(8,128)(2,1)} %bitcast.1) | data formatting | bytes 33554432
  291.4 321.0 %while.18 = (s32[]{:T(128)}, f32[1024,256]{1,0:T(8,128)S(1)}, s32[512]{0:T(512)}, s32[]{:T(128)}, s32[512]{0:T(512)}, /*index=5*/s32[]{:T(128)}, bf16[2048,256]{...) while((s32[]{:T(128)}, f32[1024,256]{1,0:T(8,128)S(1)}, ...), condition=%wide.region_7.8_spmd.clone, body=%wide.region_5.7_spmd.clone.sunk | while | flops 416057216 | bytes 28354028 | solution.py:94
  292.8 0.9 fusion.42
  293.7 0.9 constant_dynamic-slice_fusion.5
  294.6 68.7 %gather_fusion = bf16[16384,256]{1,0:T(8,128)(2,1)} fusion(bf16[32768,256]{1,0:T(8,128)(2,1)} %get-tuple-element.617, s32[16384]{0:T(1024)S(1)} %broadcast_clamp_fusion.2), kind=kCustom, calls=%fused_computation.1.clone.clone.1 | custom fusion | bytes 16842752 | tf_op jit(solution)/shard_map/while/body/eval_jaxpr/gather | solution.py:34
  363.3 5.5 fusion.43
  368.8 0.8 compare_select_fusion.4
  369.6 0.8 gather_fusion.1
  370.4 1.2 convolution_add_fusion.2
  373.1 0.9 fusion.42
  373.9 0.9 constant_dynamic-slice_fusion.5
  374.9 68.7 %gather_fusion = bf16[16384,256]{1,0:T(8,128)(2,1)} fusion(bf16[32768,256]{1,0:T(8,128)(2,1)} %get-tuple-element.617, s32[16384]{0:T(1024)S(1)} %broadcast_clamp_fusion.2), kind=kCustom, calls=%fused_computation.1.clone.clone.1 | custom fusion | bytes 16842752 | tf_op jit(solution)/shard_map/while/body/eval_jaxpr/gather | solution.py:34
  443.5 5.5 fusion.43
  449.8 0.8 gather_fusion.1
  450.6 1.2 convolution_add_fusion.2
  453.3 0.9 fusion.42
  454.1 0.9 constant_dynamic-slice_fusion.5
  455.1 68.7 %gather_fusion = bf16[16384,256]{1,0:T(8,128)(2,1)} fusion(bf16[32768,256]{1,0:T(8,128)(2,1)} %get-tuple-element.617, s32[16384]{0:T(1024)S(1)} %broadcast_clamp_fusion.2), kind=kCustom, calls=%fused_computation.1.clone.clone.1 | custom fusion | bytes 16842752 | tf_op jit(solution)/shard_map/while/body/eval_jaxpr/gather | solution.py:34
  523.7 5.5 fusion.43
  530.0 0.8 gather_fusion.1
  530.8 1.2 convolution_add_fusion.2
  533.5 0.9 fusion.42
  534.3 0.9 constant_dynamic-slice_fusion.5
  535.3 68.7 %gather_fusion = bf16[16384,256]{1,0:T(8,128)(2,1)} fusion(bf16[32768,256]{1,0:T(8,128)(2,1)} %get-tuple-element.617, s32[16384]{0:T(1024)S(1)} %broadcast_clamp_fusion.2), kind=kCustom, calls=%fused_computation.1.clone.clone.1 | custom fusion | bytes 16842752 | tf_op jit(solution)/shard_map/while/body/eval_jaxpr/gather | solution.py:34
  603.9 5.5 fusion.43
  610.2 0.8 gather_fusion.1
  611.1 1.2 convolution_add_fusion.2
  612.4 1.3 copy.45
  613.8 15.2 %fusion.11 = f32[256,256]{0,1:T(8,128)S(1)} fusion(bf16[32768,256]{0,1:T(8,128)(2,1)} %bitcast.1, f32[256,256]{0,1:T(8,128)} %all-reduce.3.cloned.1.call-done), kind=kOutput, calls=%fused_computation.25 | convolution fusion | flops 4295163904 | bytes 17301504 | tf_op jit(solution)/shard_map/dot_general | solution.py:28
  629.2 11.7 %cholesky.50 = f32[128,128]{1,0:T(8,128)S(1)} custom-call(f32[128,128]{1,0:T(8,128)S(1)} %cholesky.118), custom_call_target="Cholesky" | custom-call | tf_op jit(solution)/shard_map/jit(cholesky)/cholesky | solution.py:96
  640.9 9.8 %custom-call.18 = f32[1,128,128]{1,2,0:T(8,128)S(1)} custom-call(f32[1,128,128]{2,1,0:T(8,128)S(1)} %get-tuple-element.463), custom_call_target="InvertDiagBlocksLowerTriangular" | custom-call | tf_op jit(solution)/shard_map/jit(cholesky)/cholesky | solution.py:96
  651.3 11.9 %cholesky.105 = f32[128,128]{1,0:T(8,128)S(1)} custom-call(f32[128,128]{1,0:T(8,128)S(1)} %convolution_subtract_fusion.2), custom_call_target="Cholesky" | custom-call | tf_op jit(solution)/shard_map/jit(cholesky)/cholesky | solution.py:96
  665.3 4.1 while.17
  666.0 1.3 bitcast_dynamic-update-slice_fusion.2
  668.0 1.3 bitcast_dynamic-update-slice_fusion.2
  669.4 19.7 %custom-call.19 = f32[2,128,128]{1,2,0:T(8,128)S(1)} custom-call(f32[2,128,128]{2,1,0:T(8,128)S(1)} %get-tuple-element.332), custom_call_target="InvertDiagBlocksLowerTriangular" | custom-call | tf_op jit(solution)/shard_map/jit(_cho_solve)/triangular_solve | solution.py:97
  689.1 1.1 fusion.13
  690.2 1.0 convolution_subtract_fusion.1
  692.3 14.1 %all_to_all.36 = f32[128,16,16]{0,2,1:T(8,128)S(1)} all-to-all(f32[128,16,16]{0,2,1:T(8,128)S(1)} %bitcast.78), channel_id=1, replica_groups=mesh['rows'=16,'cols'=8] {'rows'}, dimensions={1} | all-to-all | bytes 262144 | tf_op jit(solution)/shard_map/all_to_all | solution.py:99
  706.5 9.2 %all_to_all.37 = f32[8,256,16]{1,2,0:T(8,128)S(1)} all-to-all(f32[8,256,16]{1,2,0:T(8,128)S(1)} %copy.47), channel_id=1, replica_groups=mesh['rows'=16,'cols'=8] {'cols'}, dimensions={0} | all-to-all | bytes 262144 | tf_op jit(solution)/shard_map/all_to_all | solution.py:98
  (61 shorter events, 14.1 us)
Async XLA Ops:
  34.6 234.4 %all-to-all-start.1 = ((bf16[16,32768,16]{1,2,0:T(8,128)(2,1)}), bf16[16,32768,16]{1,2,0:T(8,128)(2,1)}, u32[]{:S(2)}, u32[]{:S(2)}) async-start(bf16[16,32768,16]{1,2,0:T(8,128)(2,1)} %stack.3), calls=%async_computation.1 | async-start | bytes 33554432 | tf_op jit(solution)/shard_map/all_to_all | solution.py:61
  42.1 172.1 %all-gather.2.cloned.1.call-start = ((), (), s32[]{:S(2)}) async-start(), calls=%async_computation.5 | async-start | bytes 1114112 | tf_op jit(solution)/shard_map/all_gather | solution.py:58
  42.9 571.0 %all-reduce.3.cloned.1.call-start = ((), (), s32[]{:S(2)}) async-start(), calls=%async_computation.6 | async-start | bytes 524288 | tf_op jit(solution)/shard_map/psum | solution.py:65
  217.0 472.1 %reduce-scatter.2.cloned.1.call-start = ((), (), s32[]{:S(2)}) async-start(), calls=%async_computation.7 | async-start | bytes 1179648 | tf_op jit(solution)/shard_map/reduce_scatter | solution.py:95
Sparse Core Ops, SparseCore 0:
  45.4 168.8 all-gather.1
  217.1 91.8 all-reduce.2
  613.9 39.4 reduce-scatter.1
